TPU v7x, 32 devices: a whole 2x2x4 slice. The times are simulated.
32 devices in a mesh: row: 4 (over y, x), col: 8 (over z, core).
Axes of the slice: x: 2, y: 2, z: 4, core: 2. Of those that a mesh axis runs over, the one named last changes fastest.
Arguments:
- basis: bfloat16 [40, 131072], P(None, ('row', 'col'))
- expand: float32 [3, 8, 40], replicated, may hold values from -1 to 1
- tiles: bfloat16 [3, 3072, 128, 128], P(None, ('row', 'col')), may hold values from -0.3125 to 0.3125
- tile_rows: int32 [3072], P(('row', 'col')), may hold values from 0 to 255, as said below
- tile_cols: int32 [3072], P(('row', 'col')), may hold values from 0 to 127
Outputs:
- new_block: float32 [8, 131072], P(None, ('row', 'col'))
- coefficients: float32 [8, 40], replicated
- factor: float32 [8, 8], replicated
Inputs may be any that keep to these rules, and one draw needn't show every extreme that they name: `tile_rows`: each device's 96 tiles come in 8 runs of 12; the row tiles of run k are 12 distinct values from k * 32 to (k + 1) * 32 - 1.
All inputs are finite; a program needn't handle non-finite values.
Results may differ from a plain program's by a relative error of at most 0.0054.
Values may be sent and summed in bfloat16 or wider, within the bound.
A program may use at most 64 MiB of HBM per device.

v0:
```python
import math
import jax
import jax.numpy as jnp
from jax import lax
from jax.sharding import PartitionSpec as P


def shards(basis, expand, tiles, tile_rows, tile_cols):
    highest = lax.Precision.HIGHEST
    row_count = lax.axis_size("row")
    col_count = lax.axis_size("col")
    krylov, length = basis.shape
    tile_size = tiles.shape[2]
    block_size = expand.shape[1]
    entries = length * row_count * col_count
    inverse_root = 1.0 / math.sqrt(entries)
    region = length // tile_size
    basis_full = basis.astype(jnp.float32)
    series = jnp.einsum("mbk,kn->mbn", expand, basis_full, precision=highest).astype(jnp.bfloat16)
    gathered = lax.all_gather(series, "row", axis=2, tiled=True)
    col_tiles = gathered.reshape(3, block_size, row_count * length // tile_size, tile_size)
    picked = jnp.take(col_tiles, tile_cols, axis=2)
    products = jnp.einsum("mtij,mbtj->bti", tiles, picked, preferred_element_type=jnp.float32)
    slot_count = col_count * region
    onehot = (tile_rows[:, None] == jnp.arange(slot_count, dtype=jnp.int32)[None, :]).astype(
        jnp.float32
    )
    partial_value = jnp.einsum("ts,bti->bsi", onehot, products, precision=highest).reshape(
        block_size, slot_count * tile_size
    )
    applied = lax.psum_scatter(partial_value, "col", scatter_dimension=1, tiled=True)
    raw_proj = jnp.dot(applied, basis_full.T, precision=highest) * inverse_root
    correlation = jnp.dot(basis_full, basis_full.T, precision=highest) / entries
    energy = jnp.dot(applied, applied.T, precision=highest)
    first_pass, correlation, energy = lax.psum((raw_proj, correlation, energy), ("row", "col"))
    second_pass = first_pass - jnp.dot(first_pass, correlation, precision=highest)
    coefficients = first_pass + second_pass
    mixed = jnp.dot(first_pass, coefficients.T, precision=highest)
    curved = jnp.dot(
        jnp.dot(coefficients, correlation, precision=highest), coefficients.T, precision=highest
    )
    gram_block = (energy - mixed - mixed.T + curved) / entries
    cleaned = applied - jnp.dot(coefficients, basis_full, precision=highest) * inverse_root
    factor = jnp.linalg.cholesky(gram_block)
    new_block = lax.linalg.triangular_solve(factor, cleaned, left_side=True, lower=True)
    return (new_block, coefficients, factor)


def solution(mesh):
    return jax.shard_map(
        shards,
        mesh=mesh,
        in_specs=(
            P(None, ("row", "col")),
            P(),
            P(None, ("row", "col"), None, None),
            P(("row", "col")),
            P(("row", "col")),
        ),
        out_specs=(P(None, ("row", "col")), P(), P()),
        check_vma=False,
    )
```

profile of v0, /device:TPU:10, one launch (start us, length us, event | category | flops | bytes accessed | tf_op | source)
XLA Modules:
  0.0 118.9 jit_solution(17451722167365213223)
XLA Ops:
  7.2 0.0 copy-start
  7.2 0.0 copy-start.2
  7.2 0.0 reduce-scatter.2.cloned.1.call-start
  7.2 0.7 compare_select_fusion
  7.9 0.7 compare_and_fusion
  8.6 0.0 copy-done
  8.6 1.0 convolution_convert_fusion
  9.6 11.2 %all_gather.3 = bf16[3,8,16384]{2,1,0:T(8,128)(2,1)S(1)} all-gather(bf16[3,8,4096]{2,1,0:T(8,128)(2,1)S(1)} %convolution_convert_fusion), channel_id=1, replica_groups=mesh['row'=4,'col'=8] {'row'}, dimensions={2}, use_global_device_ids=true | all-gather | bytes 983040 | tf_op jit(solution)/shard_map/all_gather | solution.py:20
  20.8 0.8 gather_fusion
  21.6 5.9 %fusion = f32[96,8,128,1]{2,1,3,0:T(8,128)S(1)} fusion(bf16[3,96,128,128]{3,2,1,0:T(8,128)(2,1)} %param.7, bf16[96,3,8,128]{3,2,1,0:T(8,128)(2,1)S(1)} %gather_fusion, pred[96]{0:T(512)(128)(4,1)S(1)} %compare_and_fusion), kind=kOutput, calls=%fused_computation.1 | convolution fusion | flops 75792384 | bytes 10420320 | tf_op jit(solution)/shard_map/mtij,mbtj->bti/dot_general | solution.py:23
  27.5 0.0 copy-done.2
  27.5 0.7 convolution_bitcast_fusion
  28.2 0.3 copy.13
  28.5 1.6 %copy.31 = f32[1,8,256,128]{3,1,2,0:T(8,128)} copy(f32[1,8,256,128]{3,2,1,0:T(8,128)S(1)} %bitcast.54) | data formatting | bytes 2097152
  30.1 0.0 reduce-scatter.2.cloned.1.call-update
  30.2 0.2 convolution_multiply_fusion.1
  30.4 29.0 %reduce-scatter.2.cloned.1.call-done = f32[8,4096]{1,0:T(8,128)} async-done(((f32[8,32768]{1,0:T(8,128)}), f32[8,4096]{1,0:T(8,128)}) %reduce-scatter.2.cloned.1.call-update) | async-done | bytes 131088 | tf_op jit(solution)/shard_map/reduce_scatter | solution.py:31
  59.4 1.3 %convolution_multiply_fusion.2 = f32[8,40]{1,0:T(8,128)S(1)} fusion(f32[8,4096]{1,0:T(8,128)} %reduce-scatter.2.cloned.1.call-done, bf16[40,4096]{1,0:T(8,128)(2,1)S(1)} %copy-done), kind=kOutput, calls=%fused_computation.12 | convolution fusion | flops 15728960 | bytes 460032 | tf_op jit(solution)/shard_map/dot_general | solution.py:32
  60.7 1.3 %fusion.19 = f32[8,8]{0,1:T(8,128)S(1)} fusion(f32[8,4096]{1,0:T(8,128)} %reduce-scatter.2.cloned.1.call-done), kind=kOutput, calls=%fused_computation.39 | convolution fusion | flops 3145728 | bytes 131328 | tf_op jit(solution)/shard_map/dot_general | solution.py:34
  62.0 43.9 %all-reduce = (f32[8,40]{1,0:T(8,128)S(1)}, f32[40,40]{1,0:T(8,128)S(1)}, f32[8,8]{0,1:T(8,128)S(1)}) all-reduce(f32[8,40]{1,0:T(8,128)S(1)} %convolution_multiply_fusion.2, f32[40,40]{1,0:T(8,128)S(1)} %convolution_multiply_fusion.1, f32[8,8]{0,1:T(8,128)S(1)} %fusion.19), channel_id=1, replica_groups=mesh['row'=4,'col'=8] {'row','col'}, use_global_device_ids=true, to_apply=%region_2.3 | all-reduce | flops 1984 | bytes 15872 | tf_op jit(solution)/shard_map/psum | solution.py:35
  105.9 0.1 fusion.3
  106.0 0.0 copy-start.1
  106.0 0.1 fusion.20
  106.2 0.1 fusion.21
  106.3 0.1 copy.15
  106.4 0.1 fusion.4
  106.5 0.1 copy.17
  106.6 0.7 cholesky.16
  107.3 0.1 select_reduce_fusion
  107.4 0.6 compare_reduce_fusion
  108.0 1.2 %select_bitcast_fusion = (f32[1,8,8]{2,1,0:T(8,128)S(1)}, f32[8,8]{1,0:T(8,128)}) fusion(f32[8,8]{1,0:T(8,128)S(1)} %cholesky.16, pred[]{:T(512)} %compare_reduce_fusion), kind=kLoop, calls=%fused_computation.30 | loop fusion | flops 256 | bytes 769 | tf_op jit(solution)/shard_map/triangular_solve | solution.py:45
  109.3 0.6 custom-call.6
  109.9 1.2 fusion.2
  111.1 1.0 fusion.15
  112.0 0.0 copy-done.1
  (2 shorter events, 0.0 us)
Async XLA Ops:
  7.2 1.4 %copy-start = (bf16[40,4096]{1,0:T(8,128)(2,1)S(1)}, bf16[40,4096]{1,0:T(8,128)(2,1)}, u32[]{:S(2)}) copy-start(bf16[40,4096]{1,0:T(8,128)(2,1)} %param.5) | copy-start | bytes 983044
  7.2 20.3 %copy-start.2 = (s32[96]{0:T(128)S(1)}, s32[96]{0:T(128)}, u32[]{:S(2)}) copy-start(s32[96]{0:T(128)} %param.8) | copy-start | bytes 1156
  7.2 52.2 %reduce-scatter.2.cloned.1.call-start = ((), (), s32[]{:S(2)}) async-start(), calls=%async_computation.1 | async-start | bytes 1179648 | tf_op jit(solution)/shard_map/reduce_scatter | solution.py:31
  106.0 6.0 %copy-start.1 = (f32[8,40]{1,0:T(8,128)}, f32[8,40]{1,0:T(8,128)S(1)}, u32[]{:S(2)}) copy-start(f32[8,40]{1,0:T(8,128)S(1)} %fusion.3) | copy-start | bytes 3844
Sparse Core Ops, SparseCore 0:
  30.3 29.0 reduce-scatter.1
where the time goes:
time: 119 us
  blocking collectives  55.1 us (46%)
  waiting for transfers between devices  29 us (24%)
  between operations  14.1 us (12%)
  matrix products  13.1 us (11%)
  other arithmetic  4.65 us (4%)
  local copies, waits for them, and re-layouts  2.88 us (2%)
    psum x1, blocking collectives, shards(): lax.psum((raw_proj, correlation, energy), ('row', 'col'))  43.9 us
    reduce_scatter x1, waiting for transfers between devices, shards(): lax.psum_scatter(partial_value, 'col', scatter_dimension=1, tiled=True)  29 us
    all_gather x1, blocking collectives, shards(): gathered = lax.all_gather(series, 'row', axis=2, tiled=True)  11.2 us
    dot_general x1, matrix products, shards(): jnp.einsum('mtij,mbtj->bti', tiles, picked, preferred_element_type=jnp.fl...  5.9 us
  transfers between devices with their start and end apart: 1, of which 1 were waited for; matrix products, arithmetic and copies ran while one was open for 0% of the time, Pallas kernels for 0%

commit v1 on v0

--- a/solution.py
+++ b/solution.py
@@ -6,6 +6,11 @@
 
 
 def shards(basis, expand, tiles, tile_rows, tile_cols):
+
+    def group_note(piece_in):
+        near = jax.lax.all_gather(piece_in, "row")
+        return jnp.concatenate(near, axis=2)
+
     highest = lax.Precision.HIGHEST
     row_count = lax.axis_size("row")
     col_count = lax.axis_size("col")
@@ -17,7 +22,7 @@
     region = length // tile_size
     basis_full = basis.astype(jnp.float32)
     series = jnp.einsum("mbk,kn->mbn", expand, basis_full, precision=highest).astype(jnp.bfloat16)
-    gathered = lax.all_gather(series, "row", axis=2, tiled=True)
+    gathered = group_note(series)
     col_tiles = gathered.reshape(3, block_size, row_count * length // tile_size, tile_size)
     picked = jnp.take(col_tiles, tile_cols, axis=2)
     products = jnp.einsum("mtij,mbtj->bti", tiles, picked, preferred_element_type=jnp.float32)

time: 119 us -> 121 us (1.017)
  local copies, waits for them, and re-layouts: 2.88 us -> 4.81 us
    another operation x0 -> x2, local copies, waits for them, and re-layouts: none -> 1.32 us  [shards(): gathered.reshape(3, block_size, row_count * length // tile_size, tile_size)]
where the time goes in v1:
time: 121 us
  blocking collectives  55.1 us (46%)
  waiting for transfers between devices  29 us (24%)
  between operations  14.1 us (12%)
  matrix products  13.1 us (11%)
  local copies, waits for them, and re-layouts  4.81 us (4%)
  other arithmetic  4.65 us (4%)
    psum x1, blocking collectives, shards(): lax.psum((raw_proj, correlation, energy), ('row', 'col'))  43.9 us
    reduce_scatter x1, waiting for transfers between devices, shards(): lax.psum_scatter(partial_value, 'col', scatter_dimension=1, tiled=True)  29 us
    all_gather x1, blocking collectives, group_note(): near = jax.lax.all_gather(piece_in, 'row')  11.2 us
    dot_general x1, matrix products, shards(): jnp.einsum('mtij,mbtj->bti', tiles, picked, preferred_element_type=jnp.fl...  5.9 us
  transfers between devices with their start and end apart: 1, of which 1 were waited for; matrix products, arithmetic and copies ran while one was open for 0% of the time, Pallas kernels for 0%

profile of v1, /device:TPU:10, one launch (start us, length us, event | category | flops | bytes accessed | tf_op | source)
XLA Modules:
  0.0 120.9 jit_solution(13950900573527171333)
XLA Ops:
  7.2 0.0 copy-start
  7.2 0.0 copy-start.2
  7.2 0.0 reduce-scatter.2.cloned.1.call-start
  7.2 0.7 compare_select_fusion
  7.9 0.7 compare_and_fusion
  8.6 0.0 copy-done
  8.6 1.0 convolution_convert_fusion
  9.6 11.2 %all-gather = bf16[12,8,4096]{2,1,0:T(8,128)(2,1)S(1)} all-gather(bf16[3,8,4096]{2,1,0:T(8,128)(2,1)S(1)} %convolution_convert_fusion), channel_id=2, replica_groups=mesh['row'=4,'col'=8] {'row'}, dimensions={0}, use_global_device_ids=true | all-gather | bytes 983040 | tf_op jit(solution)/shard_map/all_gather | solution.py:11
  20.8 0.6 copy.44
  21.4 0.8 reshape_reshape.3
  22.2 0.5 copy.22
  22.8 0.8 gather_fusion
  23.6 5.9 %fusion.3 = f32[8,96,128]{2,0,1:T(8,128)S(1)} fusion(bf16[3,96,128,128]{3,2,1,0:T(8,128)(2,1)} %param.7, bf16[96,3,8,128]{3,2,1,0:T(8,128)(2,1)S(1)} %gather_fusion, pred[96]{0:T(512)(128)(4,1)S(1)} %compare_and_fusion), kind=kOutput, calls=%fused_computation.7 | convolution fusion | flops 75792384 | bytes 10420320 | tf_op jit(solution)/shard_map/mtij,mbtj->bti/dot_general | solution.py:28
  29.5 0.0 copy-done.2
  29.5 0.7 convolution_bitcast_fusion
  30.2 0.3 copy.25
  30.5 1.6 %copy.43 = f32[1,8,256,128]{3,1,2,0:T(8,128)} copy(f32[1,8,256,128]{3,2,1,0:T(8,128)S(1)} %bitcast.57) | data formatting | bytes 2097152
  32.1 0.0 reduce-scatter.2.cloned.1.call-update
  32.1 0.2 convolution_multiply_fusion.1
  32.3 29.0 %reduce-scatter.2.cloned.1.call-done = f32[8,4096]{1,0:T(8,128)} async-done(((f32[8,32768]{1,0:T(8,128)}), f32[8,4096]{1,0:T(8,128)}) %reduce-scatter.2.cloned.1.call-update) | async-done | bytes 131088 | tf_op jit(solution)/shard_map/reduce_scatter | solution.py:36
  61.3 1.3 %convolution_multiply_fusion.2 = f32[8,40]{1,0:T(8,128)S(1)} fusion(f32[8,4096]{1,0:T(8,128)} %reduce-scatter.2.cloned.1.call-done, bf16[40,4096]{1,0:T(8,128)(2,1)S(1)} %copy-done), kind=kOutput, calls=%fused_computation.13 | convolution fusion | flops 15728960 | bytes 460032 | tf_op jit(solution)/shard_map/dot_general | solution.py:37
  62.6 1.3 %fusion.21 = f32[8,8]{0,1:T(8,128)S(1)} fusion(f32[8,4096]{1,0:T(8,128)} %reduce-scatter.2.cloned.1.call-done), kind=kOutput, calls=%fused_computation.40 | convolution fusion | flops 3145728 | bytes 131328 | tf_op jit(solution)/shard_map/dot_general | solution.py:39
  63.9 43.9 %all-reduce = (f32[8,40]{1,0:T(8,128)S(1)}, f32[40,40]{1,0:T(8,128)S(1)}, f32[8,8]{0,1:T(8,128)S(1)}) all-reduce(f32[8,40]{1,0:T(8,128)S(1)} %convolution_multiply_fusion.2, f32[40,40]{1,0:T(8,128)S(1)} %convolution_multiply_fusion.1, f32[8,8]{0,1:T(8,128)S(1)} %fusion.21), channel_id=1, replica_groups=mesh['row'=4,'col'=8] {'row','col'}, use_global_device_ids=true, to_apply=%region_2.3 | all-reduce | flops 1984 | bytes 15872 | tf_op jit(solution)/shard_map/psum | solution.py:40
  107.9 0.1 fusion.6
  108.0 0.0 copy-start.1
  108.0 0.1 fusion.22
  108.2 0.1 fusion.23
  108.3 0.1 copy.27
  108.4 0.1 fusion.7
  108.5 0.1 copy.29
  108.6 0.7 cholesky.16
  109.3 0.1 select_reduce_fusion
  109.4 0.6 compare_reduce_fusion
  110.0 1.2 %select_bitcast_fusion = (f32[1,8,8]{2,1,0:T(8,128)S(1)}, f32[8,8]{1,0:T(8,128)}) fusion(f32[8,8]{1,0:T(8,128)S(1)} %cholesky.16, pred[]{:T(512)} %compare_reduce_fusion), kind=kLoop, calls=%fused_computation.31 | loop fusion | flops 256 | bytes 769 | tf_op jit(solution)/shard_map/triangular_solve | solution.py:50
  111.2 0.6 custom-call.6
  111.9 1.2 fusion.2
  113.0 1.0 fusion.17
  114.0 0.0 copy-done.1
  (2 shorter events, 0.0 us)
Async XLA Ops:
  7.2 1.4 %copy-start = (bf16[40,4096]{1,0:T(8,128)(2,1)S(1)}, bf16[40,4096]{1,0:T(8,128)(2,1)}, u32[]{:S(2)}) copy-start(bf16[40,4096]{1,0:T(8,128)(2,1)} %param.5) | copy-start | bytes 983044
  7.2 22.3 %copy-start.2 = (s32[96]{0:T(128)S(1)}, s32[96]{0:T(128)}, u32[]{:S(2)}) copy-start(s32[96]{0:T(128)} %param.8) | copy-start | bytes 1156
  7.2 54.1 %reduce-scatter.2.cloned.1.call-start = ((), (), s32[]{:S(2)}) async-start(), calls=%async_computation.1 | async-start | bytes 1179648 | tf_op jit(solution)/shard_map/reduce_scatter | solution.py:36
  108.0 6.0 %copy-start.1 = (f32[8,40]{1,0:T(8,128)}, f32[8,40]{1,0:T(8,128)S(1)}, u32[]{:S(2)}) copy-start(f32[8,40]{1,0:T(8,128)S(1)} %fusion.6) | copy-start | bytes 3844
Sparse Core Ops, SparseCore 0:
  32.2 29.0 reduce-scatter.1

commit v2 on v0

--- a/solution.py
+++ b/solution.py
@@ -3,6 +3,11 @@
 import jax.numpy as jnp
 from jax import lax
 from jax.sharding import PartitionSpec as P
+
+
+def divide_skins(buf, axis_id, net_axis):
+    r_now = lax.psum(lax.psum(buf, axis_name=axis_id), axis_name=net_axis)
+    return r_now
 
 
 def shards(basis, expand, tiles, tile_rows, tile_cols):
@@ -32,7 +37,7 @@
     raw_proj = jnp.dot(applied, basis_full.T, precision=highest) * inverse_root
     correlation = jnp.dot(basis_full, basis_full.T, precision=highest) / entries
     energy = jnp.dot(applied, applied.T, precision=highest)
-    first_pass, correlation, energy = lax.psum((raw_proj, correlation, energy), ("row", "col"))
+    first_pass, correlation, energy = divide_skins((raw_proj, correlation, energy), "col", "row")
     second_pass = first_pass - jnp.dot(first_pass, correlation, precision=highest)
     coefficients = first_pass + second_pass
     mixed = jnp.dot(first_pass, coefficients.T, precision=highest)

time: 119 us -> 123 us (1.034)
  the two profiles are of different devices: /device:TPU:10 before, /device:TPU:0 now
where the time goes in v2:
time: 123 us
  blocking collectives  55.3 us (45%)
  waiting for transfers between devices  32.9 us (27%)
  between operations  14.1 us (11%)
  matrix products  13.1 us (11%)
  other arithmetic  4.65 us (4%)
  local copies, waits for them, and re-layouts  2.88 us (2%)
    psum x2, blocking collectives, divide_skins(): r_now = lax.psum(lax.psum(buf, axis_name=axis_id), axis_name=net_axis)  42.7 us
    reduce_scatter x1, waiting for transfers between devices, shards(): lax.psum_scatter(partial_value, 'col', scatter_dimension=1, tiled=True)  32.8 us
    all_gather x1, blocking collectives, shards(): gathered = lax.all_gather(series, 'row', axis=2, tiled=True)  12.7 us
    dot_general x1, matrix products, shards(): jnp.einsum('mtij,mbtj->bti', tiles, picked, preferred_element_type=jnp.fl...  5.9 us
  transfers between devices with their start and end apart: 1, of which 1 were waited for; matrix products, arithmetic and copies ran while one was open for 0% of the time, Pallas kernels for 0%

profile of v2, /device:TPU:0, one launch (start us, length us, event | category | flops | bytes accessed | tf_op | source)
XLA Modules:
  0.0 123.0 jit_solution(13946684138139590406)
XLA Ops:
  7.2 0.0 copy-start
  7.2 0.0 copy-start.2
  7.2 0.0 reduce-scatter.2.cloned.1.call-start
  7.2 0.7 compare_select_fusion
  7.9 0.7 compare_and_fusion
  8.6 0.0 copy-done
  8.6 1.0 convolution_convert_fusion
  9.6 12.7 %all_gather.3 = bf16[3,8,16384]{2,1,0:T(8,128)(2,1)S(1)} all-gather(bf16[3,8,4096]{2,1,0:T(8,128)(2,1)S(1)} %convolution_convert_fusion), channel_id=1, replica_groups=mesh['row'=4,'col'=8] {'row'}, dimensions={2}, use_global_device_ids=true | all-gather | bytes 983040 | tf_op jit(solution)/shard_map/all_gather | solution.py:25
  22.3 0.8 gather_fusion
  23.1 5.9 %fusion = f32[96,8,128,1]{2,1,3,0:T(8,128)S(1)} fusion(bf16[3,96,128,128]{3,2,1,0:T(8,128)(2,1)} %param.7, bf16[96,3,8,128]{3,2,1,0:T(8,128)(2,1)S(1)} %gather_fusion, pred[96]{0:T(512)(128)(4,1)S(1)} %compare_and_fusion), kind=kOutput, calls=%fused_computation.1 | convolution fusion | flops 75792384 | bytes 10420320 | tf_op jit(solution)/shard_map/mtij,mbtj->bti/dot_general | solution.py:28
  29.0 0.0 copy-done.2
  29.0 0.7 convolution_bitcast_fusion
  29.7 0.3 copy.13
  30.0 1.6 %copy.31 = f32[1,8,256,128]{3,1,2,0:T(8,128)} copy(f32[1,8,256,128]{3,2,1,0:T(8,128)S(1)} %bitcast.54) | data formatting | bytes 2097152
  31.6 0.0 reduce-scatter.2.cloned.1.call-update
  31.6 0.2 convolution_multiply_fusion.1
  31.9 32.8 %reduce-scatter.2.cloned.1.call-done = f32[8,4096]{1,0:T(8,128)} async-done(((f32[8,32768]{1,0:T(8,128)}), f32[8,4096]{1,0:T(8,128)}) %reduce-scatter.2.cloned.1.call-update) | async-done | bytes 131088 | tf_op jit(solution)/shard_map/reduce_scatter | solution.py:36
  64.7 1.3 %convolution_multiply_fusion.2 = f32[8,40]{1,0:T(8,128)S(1)} fusion(f32[8,4096]{1,0:T(8,128)} %reduce-scatter.2.cloned.1.call-done, bf16[40,4096]{1,0:T(8,128)(2,1)S(1)} %copy-done), kind=kOutput, calls=%fused_computation.12 | convolution fusion | flops 15728960 | bytes 460032 | tf_op jit(solution)/shard_map/dot_general | solution.py:37
  66.0 1.3 %fusion.19 = f32[8,8]{0,1:T(8,128)S(1)} fusion(f32[8,4096]{1,0:T(8,128)} %reduce-scatter.2.cloned.1.call-done), kind=kOutput, calls=%fused_computation.39 | convolution fusion | flops 3145728 | bytes 131328 | tf_op jit(solution)/shard_map/dot_general | solution.py:39
  67.3 26.0 %all-reduce = (f32[8,40]{1,0:T(8,128)S(1)}, f32[40,40]{1,0:T(8,128)S(1)}, f32[8,8]{0,1:T(8,128)S(1)}) all-reduce(f32[8,40]{1,0:T(8,128)S(1)} %convolution_multiply_fusion.2, f32[40,40]{1,0:T(8,128)S(1)} %convolution_multiply_fusion.1, f32[8,8]{0,1:T(8,128)S(1)} %fusion.19), channel_id=1, replica_groups=mesh['row'=4,'col'=8] {'col'}, use_global_device_ids=true, to_apply=%region_3.4 | all-reduce | flops 1984 | bytes 15872 | tf_op jit(solution)/shard_map/psum | solution.py:9
  93.3 16.6 %all-reduce.1 = (f32[8,40]{1,0:T(8,128)S(1)}, f32[40,40]{1,0:T(8,128)S(1)}, f32[8,8]{0,1:T(8,128)S(1)}) all-reduce(f32[8,40]{1,0:T(8,128)S(1)} %get-tuple-element.3, f32[40,40]{1,0:T(8,128)S(1)} %get-tuple-element.4, f32[8,8]{0,1:T(8,128)S(1)} %get-tuple-element.5), channel_id=1, replica_groups=mesh['row'=4,'col'=8] {'row'}, use_global_device_ids=true, to_apply=%region_4.5 | all-reduce | flops 1984 | bytes 15872 | tf_op jit(solution)/shard_map/psum | solution.py:9
  110.0 0.1 fusion.3
  110.1 0.0 copy-start.1
  110.1 0.1 fusion.20
  110.2 0.1 fusion.21
  110.4 0.1 copy.15
  110.5 0.1 fusion.4
  110.6 0.1 copy.17
  110.7 0.7 cholesky.16
  111.4 0.1 select_reduce_fusion
  111.4 0.6 compare_reduce_fusion
  112.1 1.2 %select_bitcast_fusion = (f32[1,8,8]{2,1,0:T(8,128)S(1)}, f32[8,8]{1,0:T(8,128)}) fusion(f32[8,8]{1,0:T(8,128)S(1)} %cholesky.16, pred[]{:T(512)} %compare_reduce_fusion), kind=kLoop, calls=%fused_computation.30 | loop fusion | flops 256 | bytes 769 | tf_op jit(solution)/shard_map/triangular_solve | solution.py:50
  113.3 0.6 custom-call.6
  114.0 1.2 fusion.2
  115.1 1.0 fusion.15
  116.1 0.0 copy-done.1
  (2 shorter events, 0.0 us)
Async XLA Ops:
  7.2 1.4 %copy-start = (bf16[40,4096]{1,0:T(8,128)(2,1)S(1)}, bf16[40,4096]{1,0:T(8,128)(2,1)}, u32[]{:S(2)}) copy-start(bf16[40,4096]{1,0:T(8,128)(2,1)} %param.5) | copy-start | bytes 983044
  7.2 21.8 %copy-start.2 = (s32[96]{0:T(128)S(1)}, s32[96]{0:T(128)}, u32[]{:S(2)}) copy-start(s32[96]{0:T(128)} %param.8) | copy-start | bytes 1156
  7.2 57.5 %reduce-scatter.2.cloned.1.call-start = ((), (), s32[]{:S(2)}) async-start(), calls=%async_computation.1 | async-start | bytes 1179648 | tf_op jit(solution)/shard_map/reduce_scatter | solution.py:36
  110.1 6.0 %copy-start.1 = (f32[8,40]{1,0:T(8,128)}, f32[8,40]{1,0:T(8,128)S(1)}, u32[]{:S(2)}) copy-start(f32[8,40]{1,0:T(8,128)S(1)} %fusion.3) | copy-start | bytes 3844
Sparse Core Ops, SparseCore 0:
  31.8 32.8 reduce-scatter.1
